TPU v7x, 32 devices: a whole 2x2x4 slice. The times are simulated.
32 devices in a mesh: tm: 16 (over z, x, core), gz: 2 (over y).
Axes of the slice: x: 2, y: 2, z: 4, core: 2. Of those that a mesh axis runs over, the one named last changes fastest.
Arguments:
- starts: float32 [16, 8, 32, 128], P('tm', 'gz'), may hold values from -6 to 6
- cell_rates: float32 [8, 32, 128], P('gz'), may hold values from 0.3 to 1
Outputs:
- slab_ends: float32 [16, 8, 32, 128], P('tm', 'gz')
- next_starts: float32 [16, 8, 32, 128], P('tm', 'gz')
All inputs are finite; a program needn't handle non-finite values.
Results may differ from a plain program's by a relative error of at most 0.0001.
Values sent between devices are 32-bit elements; how exact they have to be, the bound alone decides.
A program may use at most 64 MiB of HBM per device.

v0:
```python
import jax
import jax.numpy as jnp
from jax import lax
from jax.sharding import PartitionSpec as P

FINE = 4


fine_along_z = (0.1, 0.12)
fine_along_x = (0.15, 0.12)
fine_along_y = (0.2, 0.12)
coarse_along_z = (0.2, 0.25)
coarse_along_x = (0.3, 0.25)
coarse_along_y = (0.4, 0.25)


def padded_2(cells, sides, width):
    for axis, dim in sides:
        count = lax.axis_size(axis)
        head = lax.slice_in_dim(cells, 0, width, axis=dim)
        tail = lax.slice_in_dim(cells, cells.shape[dim] - width, cells.shape[dim], axis=dim)
        cells = jnp.concatenate(
            [
                lax.ppermute(tail, axis, [(i, (i + 1) % count) for i in range(count)]),
                cells,
                lax.ppermute(head, axis, [((i + 1) % count, i) for i in range(count)]),
            ],
            axis=dim,
        )
    return cells


def shifted(shard, axis, by):
    size = lax.axis_size(axis)
    return lax.ppermute(shard, axis, [(i, (i + by) % size) for i in range(size)])


def line_filter(behind, middle, beyond, courant, diffuse):
    return (
        (diffuse + 0.5 * courant) * behind
        + (1.0 - 2.0 * diffuse) * middle
        + (diffuse - 0.5 * courant) * beyond
    )


def plane_filter(values, along_x, along_y):
    mixed = line_filter(
        jnp.roll(values, 1, 2), values, jnp.roll(values, -1, 2), along_y[0], along_y[1]
    )
    return line_filter(jnp.roll(mixed, 1, 1), mixed, jnp.roll(mixed, -1, 1), along_x[0], along_x[1])


def depth_filter(padded, along_z):
    return line_filter(padded[:-2], padded[1:-1], padded[2:], along_z[0], along_z[1])


def restrict(values):
    extent_z, extent_x, extent_y = values.shape
    blocks = values.reshape(extent_z // 2, 2, extent_x // 2, 2, extent_y // 2, 2)
    return jnp.mean(blocks, axis=(1, 3, 5))


def prolong(values):
    extent_z, extent_x, extent_y = values.shape
    spread = jnp.broadcast_to(
        values[:, None, :, None, :, None], (extent_z, 2, extent_x, 2, extent_y, 2)
    )
    return spread.reshape(extent_z * 2, extent_x * 2, extent_y * 2)


def coarse_step(coarse, coarse_rates):
    padded = padded_2(coarse, (("gz", 0),), 1)
    mixed = depth_filter(plane_filter(padded, coarse_along_x, coarse_along_y), coarse_along_z)
    return coarse + coarse_rates * (mixed - coarse)


def per_device(starts, cell_rates):
    start = starts[0]
    coarse_rates = restrict(cell_rates)
    fine_end = start
    for sweep_index in range(FINE):
        padded = padded_2(fine_end, (("gz", 0),), 1)
        mixed = depth_filter(plane_filter(padded, fine_along_x, fine_along_y), fine_along_z)
        fine_end = fine_end + cell_rates * (mixed - fine_end)
    correction = fine_end - prolong(coarse_step(restrict(start), coarse_rates))
    my_index = lax.axis_index("tm")
    links = lax.axis_size("tm") - 1
    all_starts, all_terms = (
        lax.all_gather(restrict(start)[None], "tm", axis=0, tiled=True),
        lax.all_gather(restrict(correction)[None], "tm", axis=0, tiled=True),
    )

    def advance(turn_index, coarse):
        term = lax.dynamic_index_in_dim(all_terms, turn_index, 0, keepdims=False)
        finish = coarse_step(coarse, coarse_rates) + term
        return jnp.where(turn_index < my_index, finish, coarse)

    coarse = lax.fori_loop(0, links, advance, all_starts[0])
    slab_end = prolong(coarse_step(coarse, coarse_rates)) + correction
    next_start = shifted(slab_end, "tm", 1)
    return (slab_end[None], next_start[None])


def solution(mesh):
    return jax.shard_map(
        per_device,
        mesh=mesh,
        in_specs=(P("tm", "gz", None, None), P("gz", None, None)),
        out_specs=(P("tm", "gz", None, None), P("tm", "gz", None, None)),
        check_vma=False,
    )
```

profile of v0, /device:TPU:0, one launch (start us, length us, event | category | flops | bytes accessed | tf_op | source)
XLA Modules:
  0.0 187.1 jit_solution(4059996338169251306)
XLA Ops:
  0.6 6.3 %reshape_squeeze.4 = f32[2,2,16,2,64,2]{5,4,3,2,1,0:T(8,128)} reshape(f32[1,4,32,128]{3,2,1,0:T(8,128)} %param.4) | data formatting | bytes 131072 | tf_op jit(solution)/shard_map/reshape;squeeze | solution.py:59
  7.0 2.5 %reduce_sum.27 = f32[2,16,64]{2,1,0:T(8,128)S(1)} reduce(f32[2,2,16,2,64,2]{5,4,3,2,1,0:T(8,128)} %reshape_squeeze.4, f32[]{:T(128)} %constant.94.clone.1), dimensions={1,3,5}, to_apply=%region_0.0 | reduce | flops 14336 | bytes 73732 | tf_op jit(solution)/shard_map/reduce_sum | solution.py:60
  9.6 3.1 %collective-permute-start.11 = (f32[1,16,64]{2,1,0:T(8,128)S(1)}, f32[1,16,64]{2,1,0:T(8,128)S(1)}, u32[]{:S(2)}, u32[]{:S(2)}) collective-permute-start(f32[1,16,64]{2,1,0:T(8,128)S(1)} %get-tuple-element.178), channel_id=1, source_target_pairs={{1,0},{0,1},{3,2},{2,3},{5,4},{4,5},{7,6},{6,7},{9,8},{8,9},{11,10... | collective-permute-start | bytes 12296 | tf_op jit(solution)/shard_map/ppermute | solution.py:26
  12.7 1.9 %collective-permute-start.3 = (f32[1,32,128]{2,1,0:T(8,128)S(1)}, f32[1,32,128]{2,1,0:T(8,128)S(1)}, u32[]{:S(2)}, u32[]{:S(2)}) collective-permute-start(f32[1,32,128]{2,1,0:T(8,128)S(1)} %get-tuple-element.156), channel_id=1, source_target_pairs={{1,0},{0,1},{3,2},{2,3},{5,4},{4,5},{7,6},{6,7},{9,8},{8,9},{11,10... | collective-permute-start | bytes 49160 | tf_op jit(solution)/shard_map/ppermute | solution.py:26
  14.7 22.7 %all-gather = f32[32,16,64]{2,1,0:T(8,128)S(1)} all-gather(f32[2,16,64]{2,1,0:T(8,128)S(1)} %broadcast_multiply_fusion.2), channel_id=2, replica_groups=mesh['tm'=16,'gz'=2] {'tm'}, dimensions={0}, use_global_device_ids=true | all-gather | bytes 139264 | tf_op jit(solution)/shard_map/all_gather | solution.py:89
  37.5 5.5 %reshape.38 = f32[2,2,16,2,64,2]{5,4,3,2,1,0:T(8,128)} reshape(f32[4,32,128]{2,1,0:T(8,128)S(1)} %copy-done.1) | data formatting | bytes 131072 | tf_op jit(solution)/shard_map/reshape | solution.py:59
  43.0 2.5 %reduce_sum.32 = f32[2,16,64]{2,1,0:T(8,128)S(1)} reduce(f32[2,2,16,2,64,2]{5,4,3,2,1,0:T(8,128)} %reshape.38, f32[]{:T(128)} %constant.94.clone.1), dimensions={1,3,5}, to_apply=%region_1.2 | reduce | flops 14336 | bytes 73732 | tf_op jit(solution)/shard_map/reduce_sum | solution.py:60
  48.4 1.7 collective-permute-done.5
  54.2 1.7 collective-permute-done.7
  59.0 2.5 %broadcast_in_dim.8 = f32[2,2,16,2,64,2]{5,4,3,2,1,0:T(8,128)} broadcast(f32[2,16,64]{2,1,0:T(8,128)S(1)} %get-tuple-element.175), dimensions={0,2,4} | broadcast | bytes 73728 | tf_op jit(solution)/shard_map/broadcast_in_dim | solution.py:65
  61.5 4.0 %reshape.39 = f32[4,32,128]{2,1,0:T(8,128)S(1)} reshape(f32[2,2,16,2,64,2]{5,4,3,2,1,0:T(8,128)} %broadcast_in_dim.8) | data formatting | bytes 131072 | tf_op jit(solution)/shard_map/reshape | solution.py:68
  66.0 5.5 %reshape.40 = f32[2,2,16,2,64,2]{5,4,3,2,1,0:T(8,128)} reshape(f32[4,32,128]{2,1,0:T(8,128)S(1)} %fusion.31) | data formatting | bytes 131072 | tf_op jit(solution)/shard_map/reshape | solution.py:59
  71.6 2.5 %reduce_sum.33 = f32[2,16,64]{2,1,0:T(8,128)S(1)} reduce(f32[2,2,16,2,64,2]{5,4,3,2,1,0:T(8,128)} %reshape.40, f32[]{:T(128)} %constant.94.clone.1), dimensions={1,3,5}, to_apply=%region_2.3 | reduce | flops 14336 | bytes 73732 | tf_op jit(solution)/shard_map/reduce_sum | solution.py:60
  74.1 17.8 %all-gather.1 = f32[32,16,64]{2,1,0:T(8,128)S(1)} all-gather(f32[2,16,64]{2,1,0:T(8,128)S(1)} %broadcast_multiply_fusion), channel_id=3, replica_groups=mesh['tm'=16,'gz'=2] {'tm'}, dimensions={0}, use_global_device_ids=true | all-gather | bytes 139264 | tf_op jit(solution)/shard_map/all_gather | solution.py:90
  92.0 76.9 %while.13 = (s32[]{:T(128)}, f32[2,16,64]{2,1,0:T(8,128)S(1)}, s32[]{:T(128)}, f32[2,16,64]{2,1,0:T(8,128)S(1)}, f32[16,2,16,64]{3,2,1,0:T(8,128)S(1)}, /*index=5*/s32[]{:T(128)}) while((s32[]{:T(128)}, f32[2,16,64]{2,1,0:T(8,128)S(1)}, s32[]{:T(128)}, f32[2,16,64]{2,1,0:T(8,128)S(1)}, f32[16,2,16,64]{3,2,1,0:T(8,128)S(1)}, ...), condition=%wide.region_4.5_spmd, body=%wide.region_3.4_spmd.sunk | while | flops 77827 | bytes 430251 | solution.py:98
  94.0 1.6 collective-permute-done
  99.6 1.6 collective-permute-done
  104.2 1.6 collective-permute-done
  109.8 1.6 collective-permute-done
  114.4 1.6 collective-permute-done
  120.0 1.6 collective-permute-done
  124.6 1.6 collective-permute-done
  130.2 1.6 collective-permute-done
  134.8 1.6 collective-permute-done
  140.4 1.6 collective-permute-done
  145.0 1.6 collective-permute-done
  150.6 1.6 collective-permute-done
  155.2 1.6 collective-permute-done
  165.3 1.6 collective-permute-done
  173.4 2.5 %broadcast_in_dim.9 = f32[2,2,16,2,64,2]{5,4,3,2,1,0:T(8,128)} broadcast(f32[2,16,64]{2,1,0:T(8,128)S(1)} %fusion.59), dimensions={0,2,4} | broadcast | bytes 73728 | tf_op jit(solution)/shard_map/broadcast_in_dim | solution.py:65
  176.0 4.0 %reshape.41 = f32[4,32,128]{2,1,0:T(8,128)S(1)} reshape(f32[2,2,16,2,64,2]{5,4,3,2,1,0:T(8,128)} %broadcast_in_dim.9) | data formatting | bytes 131072 | tf_op jit(solution)/shard_map/reshape | solution.py:68
  180.1 6.4 %collective-permute-done.14 = f32[4,32,128]{2,1,0:T(8,128)S(1)} collective-permute-done((f32[4,32,128]{2,1,0:T(8,128)S(1)}, f32[4,32,128]{2,1,0:T(8,128)S(1)}, u32[]{:S(2)}, u32[]{:S(2)}) %collective-permute-start.14) | collective-permute-done | bytes 65568 | tf_op jit(solution)/shard_map/ppermute | solution.py:35
  (302 shorter events, 68.8 us)
Async XLA Ops:
  9.6 36.0 %collective-permute-start.11 = (f32[1,16,64]{2,1,0:T(8,128)S(1)}, f32[1,16,64]{2,1,0:T(8,128)S(1)}, u32[]{:S(2)}, u32[]{:S(2)}) collective-permute-start(f32[1,16,64]{2,1,0:T(8,128)S(1)} %get-tuple-element.178), channel_id=1, source_target_pairs={{1,0},{0,1},{3,2},{2,3},{5,4},{4,5},{7,6},{6,7},{9,8},{8,9},{11,10... | collective-permute-start | bytes 12296 | tf_op jit(solution)/shard_map/ppermute | solution.py:26
  12.6 32.9 %collective-permute-start.10 = (f32[1,16,64]{2,1,0:T(8,128)S(1)}, f32[1,16,64]{2,1,0:T(8,128)S(1)}, u32[]{:S(2)}, u32[]{:S(2)}) collective-permute-start(f32[1,16,64]{2,1,0:T(8,128)S(1)} %get-tuple-element.177), channel_id=1, source_target_pairs={{0,1},{1,0},{2,3},{3,2},{4,5},{5,4},{6,7},{7,6},{8,9},{9,8},{10,11... | collective-permute-start | bytes 12296 | tf_op jit(solution)/shard_map/ppermute | solution.py:24
  12.7 33.1 %collective-permute-start.3 = (f32[1,32,128]{2,1,0:T(8,128)S(1)}, f32[1,32,128]{2,1,0:T(8,128)S(1)}, u32[]{:S(2)}, u32[]{:S(2)}) collective-permute-start(f32[1,32,128]{2,1,0:T(8,128)S(1)} %get-tuple-element.156), channel_id=1, source_target_pairs={{1,0},{0,1},{3,2},{2,3},{5,4},{4,5},{7,6},{6,7},{9,8},{8,9},{11,10... | collective-permute-start | bytes 49160 | tf_op jit(solution)/shard_map/ppermute | solution.py:26
  14.6 31.2 %collective-permute-start.2 = (f32[1,32,128]{2,1,0:T(8,128)S(1)}, f32[1,32,128]{2,1,0:T(8,128)S(1)}, u32[]{:S(2)}, u32[]{:S(2)}) collective-permute-start(f32[1,32,128]{2,1,0:T(8,128)S(1)} %get-tuple-element.155), channel_id=1, source_target_pairs={{0,1},{1,0},{2,3},{3,2},{4,5},{5,4},{6,7},{7,6},{8,9},{9,8},{10,11... | collective-permute-start | bytes 49160 | tf_op jit(solution)/shard_map/ppermute | solution.py:24
  46.3 3.8 %collective-permute-start.5 = (f32[1,32,128]{2,1,0:T(8,128)S(1)}, f32[1,32,128]{2,1,0:T(8,128)S(1)}, u32[]{:S(2)}, u32[]{:S(2)}) collective-permute-start(f32[1,32,128]{2,1,0:T(8,128)S(1)} %get-tuple-element.154), channel_id=1, source_target_pairs={{1,0},{0,1},{3,2},{2,3},{5,4},{4,5},{7,6},{6,7},{9,8},{8,9},{11,10... | collective-permute-start | bytes 49160 | tf_op jit(solution)/shard_map/ppermute | solution.py:26
  47.9 3.7 %collective-permute-start.4 = (f32[1,32,128]{2,1,0:T(8,128)S(1)}, f32[1,32,128]{2,1,0:T(8,128)S(1)}, u32[]{:S(2)}, u32[]{:S(2)}) collective-permute-start(f32[1,32,128]{2,1,0:T(8,128)S(1)} %get-tuple-element.153), channel_id=1, source_target_pairs={{0,1},{1,0},{2,3},{3,2},{4,5},{5,4},{6,7},{7,6},{8,9},{9,8},{10,11... | collective-permute-start | bytes 49160 | tf_op jit(solution)/shard_map/ppermute | solution.py:24
  52.1 3.8 %collective-permute-start.7 = (f32[1,32,128]{2,1,0:T(8,128)S(1)}, f32[1,32,128]{2,1,0:T(8,128)S(1)}, u32[]{:S(2)}, u32[]{:S(2)}) collective-permute-start(f32[1,32,128]{2,1,0:T(8,128)S(1)} %get-tuple-element.152), channel_id=1, source_target_pairs={{1,0},{0,1},{3,2},{2,3},{5,4},{4,5},{7,6},{6,7},{9,8},{8,9},{11,10... | collective-permute-start | bytes 49160 | tf_op jit(solution)/shard_map/ppermute | solution.py:26
  52.7 3.7 %collective-permute-start.6 = (f32[1,32,128]{2,1,0:T(8,128)S(1)}, f32[1,32,128]{2,1,0:T(8,128)S(1)}, u32[]{:S(2)}, u32[]{:S(2)}) collective-permute-start(f32[1,32,128]{2,1,0:T(8,128)S(1)} %get-tuple-element.151), channel_id=1, source_target_pairs={{0,1},{1,0},{2,3},{3,2},{4,5},{5,4},{6,7},{7,6},{8,9},{9,8},{10,11... | collective-permute-start | bytes 49160 | tf_op jit(solution)/shard_map/ppermute | solution.py:24
  56.9 8.7 %collective-permute-start.9 = (f32[1,32,128]{2,1,0:T(8,128)S(1)}, f32[1,32,128]{2,1,0:T(8,128)S(1)}, u32[]{:S(2)}, u32[]{:S(2)}) collective-permute-start(f32[1,32,128]{2,1,0:T(8,128)S(1)} %get-tuple-element.150), channel_id=1, source_target_pairs={{1,0},{0,1},{3,2},{2,3},{5,4},{4,5},{7,6},{6,7},{9,8},{8,9},{11,10... | collective-permute-start | bytes 49160 | tf_op jit(solution)/shard_map/ppermute | solution.py:26
  58.5 7.1 %collective-permute-start.8 = (f32[1,32,128]{2,1,0:T(8,128)S(1)}, f32[1,32,128]{2,1,0:T(8,128)S(1)}, u32[]{:S(2)}, u32[]{:S(2)}) collective-permute-start(f32[1,32,128]{2,1,0:T(8,128)S(1)} %get-tuple-element.149), channel_id=1, source_target_pairs={{0,1},{1,0},{2,3},{3,2},{4,5},{5,4},{6,7},{7,6},{8,9},{9,8},{10,11... | collective-permute-start | bytes 49160 | tf_op jit(solution)/shard_map/ppermute | solution.py:24
  97.5 3.7 %collective-permute-start = (f32[1,16,64]{2,1,0:T(8,128)S(1)}, f32[1,16,64]{2,1,0:T(8,128)S(1)}, u32[]{:S(2)}, u32[]{:S(2)}) collective-permute-start(f32[1,16,64]{2,1,0:T(8,128)S(1)} %get-tuple-element.220), channel_id=1, source_target_pairs={{0,1},{1,0},{2,3},{3,2},{4,5},{5,4},{6,7},{7,6},{8,9},{9,8},{10,11... | collective-permute-start | bytes 12296 | tf_op jit(solution)/shard_map/while/body/eval_jaxpr/ppermute | solution.py:24
  98.1 3.7 %collective-permute-start.1 = (f32[1,16,64]{2,1,0:T(8,128)S(1)}, f32[1,16,64]{2,1,0:T(8,128)S(1)}, u32[]{:S(2)}, u32[]{:S(2)}) collective-permute-start(f32[1,16,64]{2,1,0:T(8,128)S(1)} %get-tuple-element.221), channel_id=1, source_target_pairs={{1,0},{0,1},{3,2},{2,3},{5,4},{4,5},{7,6},{6,7},{9,8},{8,9},{11,10... | collective-permute-start | bytes 12296 | tf_op jit(solution)/shard_map/while/body/eval_jaxpr/ppermute | solution.py:26
  102.1 3.7 %collective-permute-start = (f32[1,16,64]{2,1,0:T(8,128)S(1)}, f32[1,16,64]{2,1,0:T(8,128)S(1)}, u32[]{:S(2)}, u32[]{:S(2)}) collective-permute-start(f32[1,16,64]{2,1,0:T(8,128)S(1)} %get-tuple-element.220), channel_id=1, source_target_pairs={{0,1},{1,0},{2,3},{3,2},{4,5},{5,4},{6,7},{7,6},{8,9},{9,8},{10,11... | collective-permute-start | bytes 12296 | tf_op jit(solution)/shard_map/while/body/eval_jaxpr/ppermute | solution.py:24
  103.7 3.7 %collective-permute-start.1 = (f32[1,16,64]{2,1,0:T(8,128)S(1)}, f32[1,16,64]{2,1,0:T(8,128)S(1)}, u32[]{:S(2)}, u32[]{:S(2)}) collective-permute-start(f32[1,16,64]{2,1,0:T(8,128)S(1)} %get-tuple-element.221), channel_id=1, source_target_pairs={{1,0},{0,1},{3,2},{2,3},{5,4},{4,5},{7,6},{6,7},{9,8},{8,9},{11,10... | collective-permute-start | bytes 12296 | tf_op jit(solution)/shard_map/while/body/eval_jaxpr/ppermute | solution.py:26
  107.7 3.7 %collective-permute-start = (f32[1,16,64]{2,1,0:T(8,128)S(1)}, f32[1,16,64]{2,1,0:T(8,128)S(1)}, u32[]{:S(2)}, u32[]{:S(2)}) collective-permute-start(f32[1,16,64]{2,1,0:T(8,128)S(1)} %get-tuple-element.220), channel_id=1, source_target_pairs={{0,1},{1,0},{2,3},{3,2},{4,5},{5,4},{6,7},{7,6},{8,9},{9,8},{10,11... | collective-permute-start | bytes 12296 | tf_op jit(solution)/shard_map/while/body/eval_jaxpr/ppermute | solution.py:24
  112.3 3.7 %collective-permute-start = (f32[1,16,64]{2,1,0:T(8,128)S(1)}, f32[1,16,64]{2,1,0:T(8,128)S(1)}, u32[]{:S(2)}, u32[]{:S(2)}) collective-permute-start(f32[1,16,64]{2,1,0:T(8,128)S(1)} %get-tuple-element.220), channel_id=1, source_target_pairs={{0,1},{1,0},{2,3},{3,2},{4,5},{5,4},{6,7},{7,6},{8,9},{9,8},{10,11... | collective-permute-start | bytes 12296 | tf_op jit(solution)/shard_map/while/body/eval_jaxpr/ppermute | solution.py:24
  113.9 3.7 %collective-permute-start.1 = (f32[1,16,64]{2,1,0:T(8,128)S(1)}, f32[1,16,64]{2,1,0:T(8,128)S(1)}, u32[]{:S(2)}, u32[]{:S(2)}) collective-permute-start(f32[1,16,64]{2,1,0:T(8,128)S(1)} %get-tuple-element.221), channel_id=1, source_target_pairs={{1,0},{0,1},{3,2},{2,3},{5,4},{4,5},{7,6},{6,7},{9,8},{8,9},{11,10... | collective-permute-start | bytes 12296 | tf_op jit(solution)/shard_map/while/body/eval_jaxpr/ppermute | solution.py:26
  117.9 3.7 %collective-permute-start = (f32[1,16,64]{2,1,0:T(8,128)S(1)}, f32[1,16,64]{2,1,0:T(8,128)S(1)}, u32[]{:S(2)}, u32[]{:S(2)}) collective-permute-start(f32[1,16,64]{2,1,0:T(8,128)S(1)} %get-tuple-element.220), channel_id=1, source_target_pairs={{0,1},{1,0},{2,3},{3,2},{4,5},{5,4},{6,7},{7,6},{8,9},{9,8},{10,11... | collective-permute-start | bytes 12296 | tf_op jit(solution)/shard_map/while/body/eval_jaxpr/ppermute | solution.py:24
  118.5 3.7 %collective-permute-start.1 = (f32[1,16,64]{2,1,0:T(8,128)S(1)}, f32[1,16,64]{2,1,0:T(8,128)S(1)}, u32[]{:S(2)}, u32[]{:S(2)}) collective-permute-start(f32[1,16,64]{2,1,0:T(8,128)S(1)} %get-tuple-element.221), channel_id=1, source_target_pairs={{1,0},{0,1},{3,2},{2,3},{5,4},{4,5},{7,6},{6,7},{9,8},{8,9},{11,10... | collective-permute-start | bytes 12296 | tf_op jit(solution)/shard_map/while/body/eval_jaxpr/ppermute | solution.py:26
  122.5 3.7 %collective-permute-start = (f32[1,16,64]{2,1,0:T(8,128)S(1)}, f32[1,16,64]{2,1,0:T(8,128)S(1)}, u32[]{:S(2)}, u32[]{:S(2)}) collective-permute-start(f32[1,16,64]{2,1,0:T(8,128)S(1)} %get-tuple-element.220), channel_id=1, source_target_pairs={{0,1},{1,0},{2,3},{3,2},{4,5},{5,4},{6,7},{7,6},{8,9},{9,8},{10,11... | collective-permute-start | bytes 12296 | tf_op jit(solution)/shard_map/while/body/eval_jaxpr/ppermute | solution.py:24
  128.1 3.7 %collective-permute-start = (f32[1,16,64]{2,1,0:T(8,128)S(1)}, f32[1,16,64]{2,1,0:T(8,128)S(1)}, u32[]{:S(2)}, u32[]{:S(2)}) collective-permute-start(f32[1,16,64]{2,1,0:T(8,128)S(1)} %get-tuple-element.220), channel_id=1, source_target_pairs={{0,1},{1,0},{2,3},{3,2},{4,5},{5,4},{6,7},{7,6},{8,9},{9,8},{10,11... | collective-permute-start | bytes 12296 | tf_op jit(solution)/shard_map/while/body/eval_jaxpr/ppermute | solution.py:24
  128.7 3.7 %collective-permute-start.1 = (f32[1,16,64]{2,1,0:T(8,128)S(1)}, f32[1,16,64]{2,1,0:T(8,128)S(1)}, u32[]{:S(2)}, u32[]{:S(2)}) collective-permute-start(f32[1,16,64]{2,1,0:T(8,128)S(1)} %get-tuple-element.221), channel_id=1, source_target_pairs={{1,0},{0,1},{3,2},{2,3},{5,4},{4,5},{7,6},{6,7},{9,8},{8,9},{11,10... | collective-permute-start | bytes 12296 | tf_op jit(solution)/shard_map/while/body/eval_jaxpr/ppermute | solution.py:26
  132.7 3.7 %collective-permute-start = (f32[1,16,64]{2,1,0:T(8,128)S(1)}, f32[1,16,64]{2,1,0:T(8,128)S(1)}, u32[]{:S(2)}, u32[]{:S(2)}) collective-permute-start(f32[1,16,64]{2,1,0:T(8,128)S(1)} %get-tuple-element.220), channel_id=1, source_target_pairs={{0,1},{1,0},{2,3},{3,2},{4,5},{5,4},{6,7},{7,6},{8,9},{9,8},{10,11... | collective-permute-start | bytes 12296 | tf_op jit(solution)/shard_map/while/body/eval_jaxpr/ppermute | solution.py:24
  134.3 3.7 %collective-permute-start.1 = (f32[1,16,64]{2,1,0:T(8,128)S(1)}, f32[1,16,64]{2,1,0:T(8,128)S(1)}, u32[]{:S(2)}, u32[]{:S(2)}) collective-permute-start(f32[1,16,64]{2,1,0:T(8,128)S(1)} %get-tuple-element.221), channel_id=1, source_target_pairs={{1,0},{0,1},{3,2},{2,3},{5,4},{4,5},{7,6},{6,7},{9,8},{8,9},{11,10... | collective-permute-start | bytes 12296 | tf_op jit(solution)/shard_map/while/body/eval_jaxpr/ppermute | solution.py:26
  138.3 3.7 %collective-permute-start = (f32[1,16,64]{2,1,0:T(8,128)S(1)}, f32[1,16,64]{2,1,0:T(8,128)S(1)}, u32[]{:S(2)}, u32[]{:S(2)}) collective-permute-start(f32[1,16,64]{2,1,0:T(8,128)S(1)} %get-tuple-element.220), channel_id=1, source_target_pairs={{0,1},{1,0},{2,3},{3,2},{4,5},{5,4},{6,7},{7,6},{8,9},{9,8},{10,11... | collective-permute-start | bytes 12296 | tf_op jit(solution)/shard_map/while/body/eval_jaxpr/ppermute | solution.py:24
  142.9 3.7 %collective-permute-start = (f32[1,16,64]{2,1,0:T(8,128)S(1)}, f32[1,16,64]{2,1,0:T(8,128)S(1)}, u32[]{:S(2)}, u32[]{:S(2)}) collective-permute-start(f32[1,16,64]{2,1,0:T(8,128)S(1)} %get-tuple-element.220), channel_id=1, source_target_pairs={{0,1},{1,0},{2,3},{3,2},{4,5},{5,4},{6,7},{7,6},{8,9},{9,8},{10,11... | collective-permute-start | bytes 12296 | tf_op jit(solution)/shard_map/while/body/eval_jaxpr/ppermute | solution.py:24
  148.5 3.7 %collective-permute-start = (f32[1,16,64]{2,1,0:T(8,128)S(1)}, f32[1,16,64]{2,1,0:T(8,128)S(1)}, u32[]{:S(2)}, u32[]{:S(2)}) collective-permute-start(f32[1,16,64]{2,1,0:T(8,128)S(1)} %get-tuple-element.220), channel_id=1, source_target_pairs={{0,1},{1,0},{2,3},{3,2},{4,5},{5,4},{6,7},{7,6},{8,9},{9,8},{10,11... | collective-permute-start | bytes 12296 | tf_op jit(solution)/shard_map/while/body/eval_jaxpr/ppermute | solution.py:24
  153.1 3.7 %collective-permute-start = (f32[1,16,64]{2,1,0:T(8,128)S(1)}, f32[1,16,64]{2,1,0:T(8,128)S(1)}, u32[]{:S(2)}, u32[]{:S(2)}) collective-permute-start(f32[1,16,64]{2,1,0:T(8,128)S(1)} %get-tuple-element.220), channel_id=1, source_target_pairs={{0,1},{1,0},{2,3},{3,2},{4,5},{5,4},{6,7},{7,6},{8,9},{9,8},{10,11... | collective-permute-start | bytes 12296 | tf_op jit(solution)/shard_map/while/body/eval_jaxpr/ppermute | solution.py:24
  158.7 3.7 %collective-permute-start = (f32[1,16,64]{2,1,0:T(8,128)S(1)}, f32[1,16,64]{2,1,0:T(8,128)S(1)}, u32[]{:S(2)}, u32[]{:S(2)}) collective-permute-start(f32[1,16,64]{2,1,0:T(8,128)S(1)} %get-tuple-element.220), channel_id=1, source_target_pairs={{0,1},{1,0},{2,3},{3,2},{4,5},{5,4},{6,7},{7,6},{8,9},{9,8},{10,11... | collective-permute-start | bytes 12296 | tf_op jit(solution)/shard_map/while/body/eval_jaxpr/ppermute | solution.py:24
  163.3 3.7 %collective-permute-start = (f32[1,16,64]{2,1,0:T(8,128)S(1)}, f32[1,16,64]{2,1,0:T(8,128)S(1)}, u32[]{:S(2)}, u32[]{:S(2)}) collective-permute-start(f32[1,16,64]{2,1,0:T(8,128)S(1)} %get-tuple-element.220), channel_id=1, source_target_pairs={{0,1},{1,0},{2,3},{3,2},{4,5},{5,4},{6,7},{7,6},{8,9},{9,8},{10,11... | collective-permute-start | bytes 12296 | tf_op jit(solution)/shard_map/while/body/eval_jaxpr/ppermute | solution.py:24
  168.9 3.7 %collective-permute-start.12 = (f32[1,16,64]{2,1,0:T(8,128)S(1)}, f32[1,16,64]{2,1,0:T(8,128)S(1)}, u32[]{:S(2)}, u32[]{:S(2)}) collective-permute-start(f32[1,16,64]{2,1,0:T(8,128)S(1)} %get-tuple-element.174), channel_id=1, source_target_pairs={{0,1},{1,0},{2,3},{3,2},{4,5},{5,4},{6,7},{7,6},{8,9},{9,8},{10,11... | collective-permute-start | bytes 12296 | tf_op jit(solution)/shard_map/ppermute | solution.py:24
  180.0 6.4 %collective-permute-start.14 = (f32[4,32,128]{2,1,0:T(8,128)S(1)}, f32[4,32,128]{2,1,0:T(8,128)S(1)}, u32[]{:S(2)}, u32[]{:S(2)}) collective-permute-start(f32[4,32,128]{2,1,0:T(8,128)S(1)} %add.249), channel_id=1, source_target_pairs={{0,2},{2,4},{4,6},{6,8},{8,10},{10,12},{12,14},{14,16},{16,18},{18... | collective-permute-start | bytes 196616 | tf_op jit(solution)/shard_map/ppermute | solution.py:35
  (16 other events, 130.2 us)
where the time goes:
time: 187 us
  waiting for transfers between devices  53.9 us (29%)
  starting transfers between devices  44.9 us (24%)
  blocking collectives  40.6 us (22%)
  local copies, waits for them, and re-layouts  34.8 us (19%)
  other arithmetic  10.8 us (6%)
    ppermute x21, waiting for transfers between devices, padded_2(): lax.ppermute(tail, axis, [(i, (i + 1) % count) for i in range(count)])  28 us
    ppermute x21, starting transfers between devices, padded_2(): lax.ppermute(head, axis, [((i + 1) % count, i) for i in range(count)])  25 us
    all_gather x1, blocking collectives, per_device(): lax.all_gather(restrict(start)[None], 'tm', axis=0, tiled=True)  22.7 us
    ppermute x21, starting transfers between devices, padded_2(): lax.ppermute(tail, axis, [(i, (i + 1) % count) for i in range(count)])  19.9 us
    ppermute x21, waiting for transfers between devices, padded_2(): lax.ppermute(head, axis, [((i + 1) % count, i) for i in range(count)])  19.5 us
    all_gather x1, blocking collectives, per_device(): lax.all_gather(restrict(correction)[None], 'tm', axis=0, tiled=True)  17.8 us
    reshape x2, local copies, waits for them, and re-layouts, restrict(): values.reshape(extent_z // 2, 2, extent_x // 2, 2, extent_y // 2, 2)  11.1 us
    reshape x2, local copies, waits for them, and re-layouts, prolong(): return spread.reshape(extent_z * 2, extent_x * 2, extent_y * 2)  8 us
  transfers between devices with their start and end apart: 43, of which 37 were waited for; matrix products, arithmetic and copies ran while one was open for 8% of the time, Pallas kernels for 0%

commit v1 on v0

v1 whole, which is shorter than its diff:
```python
import functools

import jax
import jax.numpy as jnp
from jax import lax
from jax.experimental import pallas as pl
from jax.experimental.pallas import tpu as pltpu
from jax.sharding import PartitionSpec as P

MESH = pl.DeviceIdType.MESH
FINE = 4

fine_along_z = (0.1, 0.12)
fine_along_x = (0.15, 0.12)
fine_along_y = (0.2, 0.12)
coarse_along_z = (0.2, 0.25)
coarse_along_x = (0.3, 0.25)
coarse_along_y = (0.4, 0.25)


def line_filter(behind, middle, beyond, along):
    courant, diffuse = along
    return (
        (diffuse + 0.5 * courant) * behind
        + (1.0 - 2.0 * diffuse) * middle
        + (diffuse - 0.5 * courant) * beyond
    )


def turned(values, by, dim):
    return pltpu.roll(values, by % values.shape[dim], dim)


def filtered(values, by, dim, along):
    return line_filter(turned(values, by, dim), values, turned(values, -by, dim), along)


def group_size(slabs):
    return next(q for q in range(1, slabs + 1) if slabs % q == 0 and q * q >= slabs)


def kernel(
    slabs, parts, starts_ref, rates_ref, end_ref, next_ref,
    state, rates, mixed, coarse_held, terms, sums, corr, corr_before,
    load_sem, z_send, z_recv, term_send, term_recv, sum_send, sum_recv, corr_send, corr_recv,
):
    depth, rows, lanes = rates_ref.shape
    layers = depth * parts
    size = group_size(slabs)
    groups = slabs // size
    coarse_layers, coarse_rows = layers // 2, rows // 2
    half = coarse_layers // 2
    me, part = lax.axis_index("tm"), lax.axis_index("gz")
    group, place = me // size, lax.rem(me, size)
    after, before = lax.rem(me + 1, slabs), lax.rem(me + slabs - 1, slabs)

    own = pl.ds(part * depth, depth)
    loads = [
        pltpu.make_async_copy(starts_ref.at[0], state.at[own], load_sem.at[0]),
        pltpu.make_async_copy(rates_ref, rates.at[own], load_sem.at[1]),
    ]
    for load in loads:
        load.start()

    def part_at(i):
        return {"tm": me, "gz": lax.rem(part + i, parts)}

    def place_at(i):
        return {"tm": group * size + lax.rem(place + i, size), "gz": part}

    def group_at(i):
        return {"tm": lax.rem(group + i, groups) * size + place, "gz": part}

    barrier = pltpu.get_barrier_semaphore()
    peers = (
        [part_at(i) for i in range(1, parts)]
        + [place_at(i) for i in range(1, size)]
        + [group_at(i) for i in range(1, groups)]
        + [{"tm": after, "gz": part}, {"tm": before, "gz": part}]
    )
    for peer in peers:
        pl.semaphore_signal(barrier, inc=1, device_id=peer, device_id_type=MESH)
    pl.semaphore_wait(barrier, len(peers))

    def remote(ref, send_sem, recv_sem, peer):
        return pltpu.make_async_remote_copy(
            src_ref=ref, dst_ref=ref, send_sem=send_sem, recv_sem=recv_sem,
            device_id=peer, device_id_type=MESH,
        )

    z_copies = []
    for which, ref in enumerate((state, rates)):
        loads[which].wait()
        for i in range(1, parts):
            copy = remote(ref.at[own], z_send.at[which, i], z_recv.at[which, i], part_at(i))
            copy.start()
            z_copies.append(copy)
    for copy in z_copies:
        copy.wait()

    even = lax.rem(lax.broadcasted_iota(jnp.int32, (coarse_rows, lanes), 1), 2) == 0

    def evens(ref, layer):
        return ref[layer, pl.ds(0, coarse_rows, stride=2), :]

    def odds(ref, layer):
        return ref[layer, pl.ds(1, coarse_rows, stride=2), :]

    def restricted(ref, layer):
        total = (evens(ref, layer) + odds(ref, layer)) + (evens(ref, layer + 1) + odds(ref, layer + 1))
        pair = total + jnp.where(even, turned(total, -1, 1), turned(total, 1, 1))
        return pair * 0.125

    weights = [restricted(rates, 2 * k) for k in range(coarse_layers)]
    stays = [1.0 - weight for weight in weights]

    def advance(coarse):
        plane = [
            filtered(filtered(c, 2, 1, coarse_along_y), 1, 0, coarse_along_x) for c in coarse
        ]
        return [
            weights[k]
            * line_filter(
                plane[k - 1], plane[k], plane[(k + 1) % coarse_layers], coarse_along_z
            )
            + stays[k] * coarse[k]
            for k in range(coarse_layers)
        ]

    def packed_into(ref, slot, coarse):
        for k in range(half):
            ref[slot, k] = jnp.where(even, coarse[k], coarse[k + half])

    def unpacked(ref, slot):
        first, second = [], []
        for k in range(half):
            both = ref[slot, k]
            first.append(jnp.where(even, both, turned(both, 1, 1)))
            second.append(jnp.where(even, turned(both, -1, 1), both))
        return first + second

    gate = jnp.where(me > 0, 1.0, 0.0)
    guess = [gate * c for c in advance([restricted(state, 2 * k) for k in range(coarse_layers)])]
    for k in range(coarse_layers):
        coarse_held[k] = guess[k]

    for _ in range(FINE):
        for k in range(layers):
            mixed[k] = filtered(filtered(state[k], 1, 1, fine_along_y), 1, 0, fine_along_x)
        for k in range(layers):
            deep = line_filter(mixed[(k - 1) % layers], mixed[k], mixed[(k + 1) % layers], fine_along_z)
            held = state[k]
            state[k] = held + rates[k] * (deep - held)

    term = [restricted(state, 2 * k) - guess[k] for k in range(coarse_layers)]
    packed_into(terms, place, term)
    copies = []
    for i in range(1, size):
        copy = remote(terms.at[place], term_send.at[i], term_recv.at[i], place_at(i))
        copy.start()
        copies.append(copy)

    shift = part * (depth // 2)
    sides = [pl.ds(0, coarse_rows, stride=2), pl.ds(1, coarse_rows, stride=2)]
    for k in range(depth):
        for side in sides:
            corr[k, side, :] = state[part * depth + k, side, :] - coarse_held[shift + k // 2]
    corr_copy = pltpu.make_async_remote_copy(
        src_ref=corr, dst_ref=corr_before, send_sem=corr_send.at[0], recv_sem=corr_recv.at[0],
        device_id={"tm": after, "gz": part}, device_id_type=MESH,
    )
    corr_copy.start()

    for copy in copies:
        copy.wait()
    run = unpacked(terms, 0)
    kept = [jnp.zeros_like(c) for c in run]
    for step in range(1, size):
        kept = [jnp.where(place == step, new, old) for new, old in zip(run, kept)]
        run = [c + t for c, t in zip(advance(run), unpacked(terms, step))]
    packed_into(sums, group, run)
    copies = []
    for i in range(1, groups):
        copy = remote(sums.at[group], sum_send.at[i], sum_recv.at[i], group_at(i))
        copy.start()
        copies.append(copy)
    corr_copy.wait()
    for copy in copies:
        copy.wait()

    turns = jnp.where(me == 0, groups, group)
    started = jnp.where(turns > 0, 1.0, 0.0)

    def pass_group(index, coarse):
        coarse = list(coarse)
        for _ in range(size):
            coarse = advance(coarse)
        return tuple(c + t for c, t in zip(coarse, unpacked(sums, index)))

    coarse = tuple(started * c for c in unpacked(sums, 0))
    coarse = lax.fori_loop(1, turns, pass_group, coarse)
    coarse = lax.fori_loop(0, place, lambda _, c: tuple(advance(list(c))), coarse)
    coarse = [c + t for c, t in zip(coarse, kept)]
    for k in range(coarse_layers):
        coarse_held[k] = coarse[k]
    for k in range(depth // 2):
        offset = coarse_held[shift + k] - restricted(corr_before, 2 * k)
        for layer in (2 * k, 2 * k + 1):
            for side in sides:
                next_ref[0, layer, side, :] = corr_before[layer, side, :] + offset
    finish = advance(coarse)
    for k in range(coarse_layers):
        coarse_held[k] = gate * finish[k]
    for k in range(depth):
        for side in sides:
            end_ref[0, k, side, :] = corr[k, side, :] + coarse_held[shift + k // 2]


def solution(mesh):
    slabs, parts = mesh.shape["tm"], mesh.shape["gz"]

    def per_device(starts, cell_rates):
        depth, rows, lanes = cell_rates.shape
        layers = depth * parts
        size = group_size(slabs)
        groups = slabs // size
        whole = (layers, rows, lanes)
        coarse = (layers // 2, rows // 2, lanes)
        packed = (layers // 4, rows // 2, lanes)
        vmem, dma = pltpu.VMEM, pltpu.SemaphoreType.DMA
        return pl.pallas_call(
            functools.partial(kernel, slabs, parts),
            out_shape=[jax.ShapeDtypeStruct(starts.shape, jnp.float32)] * 2,
            in_specs=[pl.BlockSpec(memory_space=pl.ANY)] * 2,
            out_specs=[pl.BlockSpec(memory_space=pltpu.VMEM)] * 2,
            scratch_shapes=[
                vmem(whole, jnp.float32),
                vmem(whole, jnp.float32),
                vmem(whole, jnp.float32),
                vmem(coarse, jnp.float32),
                vmem((size,) + packed, jnp.float32),
                vmem((groups,) + packed, jnp.float32),
                vmem((depth, rows, lanes), jnp.float32),
                vmem((depth, rows, lanes), jnp.float32),
                dma((2,)),
                dma((2, parts)),
                dma((2, parts)),
                dma((size,)),
                dma((size,)),
                dma((groups,)),
                dma((groups,)),
                dma((1,)),
                dma((1,)),
            ],
            compiler_params=pltpu.CompilerParams(collective_id=0, has_side_effects=True),
        )(starts, cell_rates)

    return jax.shard_map(
        per_device,
        mesh=mesh,
        in_specs=(P("tm", "gz", None, None), P("gz", None, None)),
        out_specs=(P("tm", "gz", None, None), P("tm", "gz", None, None)),
        check_vma=False,
    )
```

time: 187 us -> 22.9 us (0.12)
  waiting for transfers between devices: 53.9 us -> 0 us
  starting transfers between devices: 44.9 us -> 0 us
  blocking collectives: 40.6 us -> 0 us
  local copies, waits for them, and re-layouts: 34.8 us -> 2.14 us
  Pallas kernels: 0 us -> 20 us
  other arithmetic: 10.8 us -> 0 us
    ppermute x43 -> x0, waiting for transfers between devices: 53.9 us -> none  [the longest x21 28 us: padded_2(): lax.ppermute(tail, axis, [(i, (i + 1) % count) for i in range(count)])]
    ppermute x43 -> x0, starting transfers between devices: 44.9 us -> none  [the longest x21 25 us: padded_2(): lax.ppermute(head, axis, [((i + 1) % count, i) for i in range(count)])]
    all_gather x2 -> x0, blocking collectives: 40.6 us -> none  [the longest x1 22.7 us: per_device(): lax.all_gather(restrict(start)[None], 'tm', axis=0, tiled=True)]
    pallas_call x0 -> x1, Pallas kernels: none -> 20 us  [per_device(): pl.pallas_call(functools.partial(kernel, slabs, parts), out_shape=[jax.Sh...]
    reshape x4 -> x0, local copies, waits for them, and re-layouts: 19.1 us -> none  [the longest x2 11.1 us: restrict(): values.reshape(extent_z // 2, 2, extent_x // 2, 2, extent_y // 2, 2)]
    reduce_sum x3 -> x0, other arithmetic: 7.63 us -> none  [restrict(): return jnp.mean(blocks, axis=(1, 3, 5))]
    another operation x1 -> x0, local copies, waits for them, and re-layouts: 6.33 us -> none  [restrict(): values.reshape(extent_z // 2, 2, extent_x // 2, 2, extent_y // 2, 2)]
    broadcast_in_dim x2 -> x0, local copies, waits for them, and re-layouts: 5.1 us -> none  [prolong(): jnp.broadcast_to(values[:, None, :, None, :, None], (extent_z, 2, extent_...]
  transfers between devices with their start and end apart: 43 -> 0, of which waited for: 37 -> 0; matrix products, arithmetic and copies ran while one was open for 8% -> 0% of each run, Pallas kernels for 0% -> 0%
where the time goes in v1:
time: 22.9 us; the launch traced here: 22.7 us
  Pallas kernels  20 us (87%)
  local copies, waits for them, and re-layouts  2.14 us (9%)
  between operations  0.65 us (3%)
    pallas_call x1, Pallas kernels, per_device(): pl.pallas_call(functools.partial(kernel, slabs, parts), out_shape=[jax.Sh...  20 us
    unnamed x4, local copies, waits for them, and re-layouts  2.14 us

profile of v1, /device:TPU:0, one launch (start us, length us, event | category | flops | bytes accessed | tf_op | source)
XLA Modules:
  0.0 22.7 jit_solution(8065401886795179044)
XLA Ops:
  0.6 20.0 %shard_map.41 = (f32[1,4,32,128]{3,2,1,0:T(8,128)}, f32[1,4,32,128]{3,2,1,0:T(8,128)}) custom-call(f32[1,4,32,128]{3,2,1,0:T(8,128)} %starts_ref.1, f32[4,32,128]{2,1,0:T(8,128)} %rates_ref.1), custom_call_target="tpu_custom_call" | custom-call | tf_op jit(solution)/shard_map/pallas_call | solution.py:231
  20.6 0.0 copy-start
  20.6 1.5 %copy.6 = f32[1,4,32,128]{3,2,1,0:T(8,128)} copy(f32[1,4,32,128]{3,2,1,0:T(8,128)} %get-tuple-element.4) | data formatting | bytes 131072
  22.1 0.0 copy-done
  22.1 0.6 %copy.7 = f32[1,4,32,128]{3,2,1,0:T(8,128)} copy(f32[1,4,32,128]{3,2,1,0:T(8,128)S(1)} %copy-done) | data formatting | bytes 131072
Async XLA Ops:
  20.6 1.5 %copy-start = (f32[1,4,32,128]{3,2,1,0:T(8,128)S(1)}, f32[1,4,32,128]{3,2,1,0:T(8,128)}, u32[]{:S(2)}) copy-start(f32[1,4,32,128]{3,2,1,0:T(8,128)} %get-tuple-element.5) | copy-start | bytes 196612

commit v2 on v1

v2 whole, which is shorter than its diff:
```python
import functools

import jax
import jax.numpy as jnp
from jax import lax
from jax.experimental import pallas as pl
from jax.experimental.pallas import tpu as pltpu
from jax.sharding import PartitionSpec as P

MESH = pl.DeviceIdType.MESH
FINE = 4

fine_along_z = (0.1, 0.12)
fine_along_x = (0.15, 0.12)
fine_along_y = (0.2, 0.12)
coarse_along_z = (0.2, 0.25)
coarse_along_x = (0.3, 0.25)
coarse_along_y = (0.4, 0.25)


def line_filter(behind, middle, beyond, along):
    courant, diffuse = along
    return (
        (diffuse + 0.5 * courant) * behind
        + (1.0 - 2.0 * diffuse) * middle
        + (diffuse - 0.5 * courant) * beyond
    )


def turned(values, by, dim):
    return pltpu.roll(values, by % values.shape[dim], dim)


def filtered(values, by, dim, along):
    return line_filter(turned(values, by, dim), values, turned(values, -by, dim), along)


def row_size(slabs):
    return next(q for q in range(1, slabs + 1) if slabs % q == 0 and q * q >= slabs)


def group_size(slabs):
    return 2 if slabs % 2 == 0 else 1


def pair_size(size, depth):
    return 2 if size % 2 == 0 and depth % 2 == 0 else 1


def kernel(
    slabs, parts, starts_ref, rates_ref, end_ref, next_ref,
    state, rates, mixed, terms, sums, corr, corr_before,
    load_sem, state_send, state_recv, rate_send, rate_recv, pass_send, pass_recv,
    term_send, term_recv, sum_send, sum_recv, corr_sem, hop_sem,
):
    depth, rows, lanes = rates_ref.shape
    layers = depth * parts
    size = group_size(slabs)
    groups = slabs // size
    pair = pair_size(size, depth)
    share = depth // pair
    coarse_layers, coarse_rows = layers // 2, rows // 2
    half = coarse_layers // 2
    me, part = lax.axis_index("tm"), lax.axis_index("gz")
    group, place = me // size, lax.rem(me, size)
    wide = row_size(slabs)
    lines = slabs // wide
    line, column = me // wide, lax.rem(me, wide)
    after = lax.rem(me + 1, slabs)

    own = pl.ds(0, depth)
    rate_load = pltpu.make_async_copy(rates_ref, rates.at[own], load_sem.at[1])
    state_load = pltpu.make_async_copy(starts_ref.at[0], state.at[own], load_sem.at[0])
    rate_load.start()
    state_load.start()

    def part_at(i):
        return {"tm": me, "gz": lax.rem(part + i, parts)}

    def place_at(i):
        return {"tm": group * size + lax.rem(place + i, size), "gz": part}

    def group_at(i):
        return {"tm": lax.rem(group + i, groups) * size + place, "gz": part}

    def signal(sem, peer):
        pl.semaphore_signal(sem, inc=1, device_id=peer, device_id_type=MESH)

    lower, upper = line > 0, line < lines - 1
    beside = jnp.where(lower, 1, 0) + jnp.where(upper, 1, 0)

    def signal_beside(sem):
        @pl.when(lower)
        def _():
            signal(sem, {"tm": me - wide, "gz": part})

        @pl.when(upper)
        def _():
            signal(sem, {"tm": me + wide, "gz": part})

    barrier = pltpu.get_barrier_semaphore()
    near = [part_at(i) for i in range(1, parts)] + [
        {"tm": line * wide + lax.rem(column + i, wide), "gz": part} for i in range(1, wide)
    ]
    for peer in near:
        signal(barrier, peer)
    signal_beside(barrier)
    pl.semaphore_wait(barrier, len(near) + beside)

    def remote(src, dst, send_sem, recv_sem, peer):
        return pltpu.make_async_remote_copy(
            src_ref=src, dst_ref=dst, send_sem=send_sem, recv_sem=recv_sem,
            device_id=peer, device_id_type=MESH,
        )

    def started(copy):
        copy.start()
        return copy

    mine = lax.rem(me, pair) * share
    partner = {"tm": me + 1 - 2 * lax.rem(me, pair), "gz": part}
    arrivals = [(parts - i) * depth for i in range(1, parts)]
    rate_load.wait()
    rate_copies = [
        started(remote(
            rates.at[pl.ds(mine, share)], rates.at[pl.ds(at + mine, share)],
            rate_send.at[i], rate_recv.at[i], part_at(i + 1),
        ))
        for i, at in enumerate(arrivals)
    ]
    state_load.wait()
    state_copies = [
        started(remote(
            state.at[own], state.at[pl.ds(at, depth)], state_send.at[i], state_recv.at[i], part_at(i + 1)
        ))
        for i, at in enumerate(arrivals)
    ]
    for turn in range(lines - 1):
        signal_beside(hop_sem.at[turn])
        pl.semaphore_wait(hop_sem.at[turn], beside)

    pass_copies = []
    for i, at in enumerate(arrivals):
        rate_copies[i].wait()
        if pair > 1:
            piece = rates.at[pl.ds(at + mine, share)]
            pass_copies.append(
                started(remote(piece, piece, pass_send.at[i], pass_recv.at[i], partner))
            )

    def spread(first, last):
        for k in range(first, last):
            mixed[k] = filtered(filtered(state[k], 1, 1, fine_along_y), 1, 0, fine_along_x)

    spread(0, depth)
    for copy in state_copies:
        copy.wait()
    spread(depth, layers)
    for copy in pass_copies:
        copy.wait()

    even = lax.rem(lax.broadcasted_iota(jnp.int32, (coarse_rows, lanes), 1), 2) == 0
    sides = [pl.ds(0, coarse_rows, stride=2), pl.ds(1, coarse_rows, stride=2)]

    def restricted(ref, layer):
        total = (ref[layer, sides[0], :] + ref[layer, sides[1], :]) + (
            ref[layer + 1, sides[0], :] + ref[layer + 1, sides[1], :]
        )
        pair_sum = total + jnp.where(even, turned(total, -1, 1), turned(total, 1, 1))
        return pair_sum * 0.125

    weights = [restricted(rates, 2 * k) for k in range(coarse_layers)]
    stays = [1.0 - weight for weight in weights]

    def advance(coarse):
        plane = [
            filtered(filtered(c, 2, 1, coarse_along_y), 1, 0, coarse_along_x) for c in coarse
        ]
        return [
            weights[k]
            * line_filter(
                plane[k - 1], plane[k], plane[(k + 1) % coarse_layers], coarse_along_z
            )
            + stays[k] * coarse[k]
            for k in range(coarse_layers)
        ]

    def packed_into(ref, slot, coarse):
        for k in range(half):
            ref[slot, k] = jnp.where(even, coarse[k], coarse[k + half])

    def unpacked(ref, slot):
        first, second = [], []
        for k in range(half):
            both = ref[slot, k]
            first.append(jnp.where(even, both, turned(both, 1, 1)))
            second.append(jnp.where(even, turned(both, -1, 1), both))
        return first + second

    gate = jnp.where(me > 0, 1.0, 0.0)
    guess = [gate * c for c in advance([restricted(state, 2 * k) for k in range(coarse_layers)])]

    for turn in range(FINE):
        if turn > 0:
            spread(0, layers)
        for k in range(layers):
            deep = line_filter(mixed[(k - 1) % layers], mixed[k], mixed[(k + 1) % layers], fine_along_z)
            held = state[k]
            state[k] = held + rates[k] * (deep - held)

    packed_into(terms, place, [restricted(state, 2 * k) - guess[k] for k in range(coarse_layers)])
    block = terms.at[place]
    copies = [
        started(remote(block, block, term_send.at[i - 1], term_recv.at[i - 1], place_at(i)))
        for i in range(1, size)
    ]
    for k in range(depth):
        for side in sides:
            corr[k, side, :] = state[k, side, :] - guess[k // 2]
    corr_copy = started(remote(corr, corr_before, corr_sem.at[0], corr_sem.at[1], {"tm": after, "gz": part}))

    for copy in copies:
        copy.wait()
    run = unpacked(terms, 0)
    kept = [jnp.zeros_like(c) for c in run]
    for step in range(1, size):
        kept = [jnp.where(place == step, new, old) for new, old in zip(run, kept)]
        run = [c + t for c, t in zip(advance(run), unpacked(terms, step))]
    packed_into(sums, group, run)
    block = sums.at[group]
    def sum_copy(i):
        return remote(block, block, sum_send.at[i - 1], sum_recv.at[i - 1], group_at(i))

    first = me == 0
    for i in reversed(range(1, groups)):
        @pl.when((group + i < groups) | ((group + i == groups) & (place == 0)))
        def _():
            sum_copy(i).start()

    corr_copy.wait()
    before_coarse = [restricted(corr_before, 2 * k) for k in range(depth // 2)]
    for i in range(1, groups):
        @pl.when((group >= i) | first)
        def _():
            sum_copy(i).wait_recv()

    turns = jnp.where(me == 0, groups, group)
    begun = jnp.where(turns > 0, 1.0, 0.0)

    def pass_group(index, coarse):
        coarse = list(coarse)
        for _ in range(size):
            coarse = advance(coarse)
        return tuple(c + t for c, t in zip(coarse, unpacked(sums, index)))

    coarse = tuple(begun * c for c in unpacked(sums, 0))
    coarse = lax.fori_loop(1, turns, pass_group, coarse)
    coarse = lax.fori_loop(0, place, lambda _, c: tuple(advance(list(c))), coarse)
    coarse = [c + t for c, t in zip(coarse, kept)]
    finish = [gate * c for c in advance(coarse)]
    for k in range(depth):
        offset = coarse[k // 2] - before_coarse[k // 2]
        for side in sides:
            next_ref[0, k, side, :] = corr_before[k, side, :] + offset
            end_ref[0, k, side, :] = corr[k, side, :] + finish[k // 2]
    for i in range(1, groups):
        @pl.when((group + i < groups) | ((group + i == groups) & (place == 0)))
        def _():
            sum_copy(i).wait_send()


def hand_out_kernel(end_ref, next_ref, end_out, next_out, sems):
    copies = [
        pltpu.make_async_copy(end_ref, end_out, sems.at[0]),
        pltpu.make_async_copy(next_ref, next_out, sems.at[1]),
    ]
    for copy in copies:
        copy.start()
    for copy in copies:
        copy.wait()


def hand_out(end, following):
    return pl.pallas_call(
        hand_out_kernel,
        out_shape=[jax.ShapeDtypeStruct(end.shape, end.dtype)] * 2,
        in_specs=[pl.BlockSpec(memory_space=pltpu.VMEM)] * 2,
        out_specs=[pl.BlockSpec(memory_space=pl.ANY)] * 2,
        scratch_shapes=[pltpu.SemaphoreType.DMA((2,))],
    )(*(pltpu.with_memory_space_constraint(x, pltpu.VMEM) for x in (end, following)))


def solution(mesh):
    slabs, parts = mesh.shape["tm"], mesh.shape["gz"]

    def per_device(starts, cell_rates):
        depth, rows, lanes = cell_rates.shape
        layers = depth * parts
        size = group_size(slabs)
        groups = slabs // size
        whole = (layers, rows, lanes)
        packed = (layers // 4, rows // 2, lanes)
        vmem, dma = pltpu.VMEM, pltpu.SemaphoreType.DMA
        ends = pl.pallas_call(
            functools.partial(kernel, slabs, parts),
            out_shape=[pltpu.VMEM(starts.shape, jnp.float32)] * 2,
            in_specs=[pl.BlockSpec(memory_space=pl.ANY)] * 2,
            out_specs=[pl.BlockSpec(memory_space=pltpu.VMEM)] * 2,
            scratch_shapes=[
                vmem(whole, jnp.float32),
                vmem(whole, jnp.float32),
                vmem(whole, jnp.float32),
                vmem((size,) + packed, jnp.float32),
                vmem((groups,) + packed, jnp.float32),
                vmem((depth, rows, lanes), jnp.float32),
                vmem((depth, rows, lanes), jnp.float32),
                dma((2,)),
            ]
            + [dma((max(parts - 1, 1),))] * 6
            + [dma((max(size - 1, 1),))] * 2
            + [dma((max(groups - 1, 1),))] * 2
            + [dma((2,)), pltpu.SemaphoreType.REGULAR((max(slabs // row_size(slabs) - 1, 1),))],
            compiler_params=pltpu.CompilerParams(collective_id=0, has_side_effects=True),
        )(starts, cell_rates)
        return hand_out(*ends)

    return jax.shard_map(
        per_device,
        mesh=mesh,
        in_specs=(P("tm", "gz", None, None), P("gz", None, None)),
        out_specs=(P("tm", "gz", None, None), P("tm", "gz", None, None)),
        check_vma=False,
    )
```

time: 22.9 us -> 18.4 us (0.80)
  Pallas kernels: 20 us -> 17.6 us
  local copies, waits for them, and re-layouts: 2.14 us -> 0 us
    pallas_call x1 -> x2, Pallas kernels: 20 us -> 17.6 us  [the longest x1 16.9 us: per_device(): pl.pallas_call(functools.partial(kernel, slabs, parts), out_shape=[pltpu....]
    unnamed x4 -> x0, local copies, waits for them, and re-layouts: 2.14 us -> none
where the time goes in v2:
time: 18.4 us; the launch traced here: 18.2 us
  Pallas kernels  17.6 us (96%)
  between operations  0.64 us (3%)
    pallas_call x1, Pallas kernels, per_device(): pl.pallas_call(functools.partial(kernel, slabs, parts), out_shape=[pltpu....  16.9 us
    pallas_call x1, Pallas kernels, hand_out(): pl.pallas_call(hand_out_kernel, out_shape=[jax.ShapeDtypeStruct(end.shape...  0.67 us

profile of v2, /device:TPU:0, one launch (start us, length us, event | category | flops | bytes accessed | tf_op | source)
XLA Modules:
  0.0 18.2 jit_solution(8176031722786730896)
XLA Ops:
  0.6 16.9 %shard_map.41 = (f32[1,4,32,128]{3,2,1,0:T(8,128)S(1)}, f32[1,4,32,128]{3,2,1,0:T(8,128)S(1)}) custom-call(f32[1,4,32,128]{3,2,1,0:T(8,128)} %starts_ref.1, f32[4,32,128]{2,1,0:T(8,128)} %rates_ref.1), custom_call_target="tpu_custom_call" | custom-call | tf_op jit(solution)/shard_map/pallas_call | solution.py:304
  17.6 0.7 %shard_map.42 = (f32[1,4,32,128]{3,2,1,0:T(8,128)}, f32[1,4,32,128]{3,2,1,0:T(8,128)}) custom-call(f32[1,4,32,128]{3,2,1,0:T(8,128)S(1)} %get-tuple-element.4.end_ref, f32[1,4,32,128]{3,2,1,0:T(8,128)S(1)} %get-tuple-element.5.next_ref), custom_call_target="tpu_custom_call" | custom-call | tf_op jit(solution)/shard_map/pallas_call | solution.py:284

commit v3 on v2

--- a/solution.py
+++ b/solution.py
@@ -41,6 +41,14 @@
 
 def group_size(slabs):
     return 2 if slabs % 2 == 0 else 1
+
+
+def rounds(lines):
+    reaches, known = [], 1
+    while known < lines:
+        reaches.append(known)
+        known *= 2
+    return reaches
 
 
 def pair_size(size, depth):
@@ -86,17 +94,18 @@
     def signal(sem, peer):
         pl.semaphore_signal(sem, inc=1, device_id=peer, device_id_type=MESH)
 
-    lower, upper = line > 0, line < lines - 1
-    beside = jnp.where(lower, 1, 0) + jnp.where(upper, 1, 0)
-
-    def signal_beside(sem):
-        @pl.when(lower)
-        def _():
-            signal(sem, {"tm": me - wide, "gz": part})
-
-        @pl.when(upper)
-        def _():
-            signal(sem, {"tm": me + wide, "gz": part})
+    def signal_beside(sem, reach):
+        for d in range(1, reach + 1):
+            @pl.when(line >= d)
+            def _():
+                signal(sem, {"tm": me - d * wide, "gz": part})
+
+            @pl.when(line + d < lines)
+            def _():
+                signal(sem, {"tm": me + d * wide, "gz": part})
+
+    def beside(reach):
+        return jnp.minimum(line, reach) + jnp.minimum(lines - 1 - line, reach)
 
     barrier = pltpu.get_barrier_semaphore()
     near = [part_at(i) for i in range(1, parts)] + [
@@ -104,8 +113,8 @@
     ]
     for peer in near:
         signal(barrier, peer)
-    signal_beside(barrier)
-    pl.semaphore_wait(barrier, len(near) + beside)
+    signal_beside(barrier, 1)
+    pl.semaphore_wait(barrier, len(near) + beside(1))
 
     def remote(src, dst, send_sem, recv_sem, peer):
         return pltpu.make_async_remote_copy(
@@ -128,36 +137,41 @@
         ))
         for i, at in enumerate(arrivals)
     ]
+    def spread(first, last):
+        for k in range(first, last):
+            mixed[k] = filtered(filtered(state[k], 1, 1, fine_along_y), 1, 0, fine_along_x)
+
     state_load.wait()
+    spread(0, depth)
     state_copies = [
         started(remote(
             state.at[own], state.at[pl.ds(at, depth)], state_send.at[i], state_recv.at[i], part_at(i + 1)
         ))
         for i, at in enumerate(arrivals)
     ]
-    for turn in range(lines - 1):
-        signal_beside(hop_sem.at[turn])
-        pl.semaphore_wait(hop_sem.at[turn], beside)
+    reaches = rounds(lines)
+    for turn, reach in enumerate(reaches):
+        signal_beside(hop_sem.at[turn], reach)
+        if turn < len(reaches) - 1:
+            pl.semaphore_wait(hop_sem.at[turn], beside(reach))
 
     pass_copies = []
     for i, at in enumerate(arrivals):
-        rate_copies[i].wait()
+        rate_copies[i].wait_recv()
         if pair > 1:
             piece = rates.at[pl.ds(at + mine, share)]
             pass_copies.append(
                 started(remote(piece, piece, pass_send.at[i], pass_recv.at[i], partner))
             )
-
-    def spread(first, last):
-        for k in range(first, last):
-            mixed[k] = filtered(filtered(state[k], 1, 1, fine_along_y), 1, 0, fine_along_x)
-
-    spread(0, depth)
+    for reach in reaches[-1:]:
+        pl.semaphore_wait(hop_sem.at[len(reaches) - 1], beside(reach))
     for copy in state_copies:
         copy.wait()
     spread(depth, layers)
     for copy in pass_copies:
         copy.wait()
+    for copy in rate_copies:
+        copy.wait_send()
 
     even = lax.rem(lax.broadcasted_iota(jnp.int32, (coarse_rows, lanes), 1), 2) == 0
     sides = [pl.ds(0, coarse_rows, stride=2), pl.ds(1, coarse_rows, stride=2)]
@@ -231,32 +245,36 @@
     def sum_copy(i):
         return remote(block, block, sum_send.at[i - 1], sum_recv.at[i - 1], group_at(i))
 
-    first = me == 0
     for i in reversed(range(1, groups)):
         @pl.when((group + i < groups) | ((group + i == groups) & (place == 0)))
         def _():
             sum_copy(i).start()
 
-    corr_copy.wait()
-    before_coarse = [restricted(corr_before, 2 * k) for k in range(depth // 2)]
-    for i in range(1, groups):
-        @pl.when((group >= i) | first)
-        def _():
-            sum_copy(i).wait_recv()
-
     turns = jnp.where(me == 0, groups, group)
     begun = jnp.where(turns > 0, 1.0, 0.0)
 
+    def take(index):
+        i = lax.rem(group - index + groups, groups) - 1
+        held = sums.at[index]
+        remote(held, held, sum_send.at[i], sum_recv.at[i], group_at(1)).wait_recv()
+
     def pass_group(index, coarse):
+        take(index)
         coarse = list(coarse)
         for _ in range(size):
             coarse = advance(coarse)
         return tuple(c + t for c, t in zip(coarse, unpacked(sums, index)))
 
+    @pl.when(group > 0)
+    def _():
+        take(0)
+
     coarse = tuple(begun * c for c in unpacked(sums, 0))
     coarse = lax.fori_loop(1, turns, pass_group, coarse)
     coarse = lax.fori_loop(0, place, lambda _, c: tuple(advance(list(c))), coarse)
     coarse = [c + t for c, t in zip(coarse, kept)]
+    corr_copy.wait()
+    before_coarse = [restricted(corr_before, 2 * k) for k in range(depth // 2)]
     finish = [gate * c for c in advance(coarse)]
     for k in range(depth):
         offset = coarse[k // 2] - before_coarse[k // 2]
@@ -319,7 +337,7 @@
             + [dma((max(parts - 1, 1),))] * 6
             + [dma((max(size - 1, 1),))] * 2
             + [dma((max(groups - 1, 1),))] * 2
-            + [dma((2,)), pltpu.SemaphoreType.REGULAR((max(slabs // row_size(slabs) - 1, 1),))],
+            + [dma((2,)), pltpu.SemaphoreType.REGULAR((max(len(rounds(slabs // row_size(slabs))), 1),))],
             compiler_params=pltpu.CompilerParams(collective_id=0, has_side_effects=True),
         )(starts, cell_rates)
         return hand_out(*ends)

time: 18.4 us -> 17.1 us (0.929)
  Pallas kernels: 17.6 us -> 16.3 us
    pallas_call x1, Pallas kernels: 16.9 us -> 15.7 us  [per_device(): pl.pallas_call(functools.partial(kernel, slabs, parts), out_shape=[pltpu....]
where the time goes in v3:
time: 17.1 us; the launch traced here: 17 us
  Pallas kernels  16.3 us (95%)
  between operations  0.64 us (4%)
    pallas_call x1, Pallas kernels, per_device(): pl.pallas_call(functools.partial(kernel, slabs, parts), out_shape=[pltpu....  15.7 us
    pallas_call x1, Pallas kernels, hand_out(): pl.pallas_call(hand_out_kernel, out_shape=[jax.ShapeDtypeStruct(end.shape...  0.67 us

profile of v3, /device:TPU:0, one launch (start us, length us, event | category | flops | bytes accessed | tf_op | source)
XLA Modules:
  0.0 17.0 jit_solution(4624993741482203730)
XLA Ops:
  0.6 15.7 %shard_map.41 = (f32[1,4,32,128]{3,2,1,0:T(8,128)S(1)}, f32[1,4,32,128]{3,2,1,0:T(8,128)S(1)}) custom-call(f32[1,4,32,128]{3,2,1,0:T(8,128)} %starts_ref.1, f32[4,32,128]{2,1,0:T(8,128)} %rates_ref.1), custom_call_target="tpu_custom_call" | custom-call | tf_op jit(solution)/shard_map/pallas_call | solution.py:322
  16.3 0.7 %shard_map.42 = (f32[1,4,32,128]{3,2,1,0:T(8,128)}, f32[1,4,32,128]{3,2,1,0:T(8,128)}) custom-call(f32[1,4,32,128]{3,2,1,0:T(8,128)S(1)} %get-tuple-element.4.end_ref, f32[1,4,32,128]{3,2,1,0:T(8,128)S(1)} %get-tuple-element.5.next_ref), custom_call_target="tpu_custom_call" | custom-call | tf_op jit(solution)/shard_map/pallas_call | solution.py:302

commit v4 on v3

--- a/solution.py
+++ b/solution.py
@@ -142,13 +142,13 @@
             mixed[k] = filtered(filtered(state[k], 1, 1, fine_along_y), 1, 0, fine_along_x)
 
     state_load.wait()
-    spread(0, depth)
     state_copies = [
         started(remote(
             state.at[own], state.at[pl.ds(at, depth)], state_send.at[i], state_recv.at[i], part_at(i + 1)
         ))
         for i, at in enumerate(arrivals)
     ]
+    spread(0, depth)
     reaches = rounds(lines)
     for turn, reach in enumerate(reaches):
         signal_beside(hop_sem.at[turn], reach)

time: 17.1 us -> 17.1 us (level)
  no operation moved by 1% of the time
where the time goes in v4:
time: 17.1 us; the launch traced here: 17 us
  Pallas kernels  16.3 us (95%)
  between operations  0.64 us (4%)
    pallas_call x1, Pallas kernels, per_device(): pl.pallas_call(functools.partial(kernel, slabs, parts), out_shape=[pltpu....  15.7 us
    pallas_call x1, Pallas kernels, hand_out(): pl.pallas_call(hand_out_kernel, out_shape=[jax.ShapeDtypeStruct(end.shape...  0.67 us

profile of v4, /device:TPU:0, one launch (start us, length us, event | category | flops | bytes accessed | tf_op | source)
XLA Modules:
  0.0 17.0 jit_solution(2210818402632210066)
XLA Ops:
  0.6 15.7 %shard_map.41 = (f32[1,4,32,128]{3,2,1,0:T(8,128)S(1)}, f32[1,4,32,128]{3,2,1,0:T(8,128)S(1)}) custom-call(f32[1,4,32,128]{3,2,1,0:T(8,128)} %starts_ref.1, f32[4,32,128]{2,1,0:T(8,128)} %rates_ref.1), custom_call_target="tpu_custom_call" | custom-call | tf_op jit(solution)/shard_map/pallas_call | solution.py:322
  16.3 0.7 %shard_map.42 = (f32[1,4,32,128]{3,2,1,0:T(8,128)}, f32[1,4,32,128]{3,2,1,0:T(8,128)}) custom-call(f32[1,4,32,128]{3,2,1,0:T(8,128)S(1)} %get-tuple-element.4.end_ref, f32[1,4,32,128]{3,2,1,0:T(8,128)S(1)} %get-tuple-element.5.next_ref), custom_call_target="tpu_custom_call" | custom-call | tf_op jit(solution)/shard_map/pallas_call | solution.py:302
